TPU v7x, 256 devices: a 4x2x16 block of a 4x16x16 slice. The times are simulated.
256 devices in a mesh: groups: 2 (over y), seq: 128 (over z, x, core).
Axes of the slice: x: 4, y: 2, z: 16, core: 2. Of those that a mesh axis runs over, the one named last changes fastest.
The devices are a block of a 4x16x16 slice.
Arguments:
- queries: bfloat16 [65536, 2048], P(('groups', 'seq')), parts along dimension 0, may hold values from -20 to 20
- keys: bfloat16 [65536, 2048], P(('groups', 'seq')), parts along dimension 0, may hold values from -20 to 20
- values: bfloat16 [65536, 2048], P(('groups', 'seq')), parts along dimension 0, may hold values from -6 to 6
- block_counts: int32 [128], P('groups'), parts along dimension 0, may hold values from 2 to 6, as said below
- last_tokens: int32 [256], P('groups'), parts along dimension 0, may hold values from 64 to 128
- pack_order: int32 [256], P('groups'), parts along dimension 0, may hold values from 0 to 127, as said below
- decode_slot: int32 [128], P('groups'), parts along dimension 0, may hold values from 0 to 63, each once
Outputs:
- attended: bfloat16 [65536, 2048], P(('groups', 'seq')), parts along dimension 0
- cache_keys: bfloat16 [256, 256, 16, 128], P(('groups', 'seq')), parts along dimension 0
- cache_values: bfloat16 [256, 256, 16, 128], P(('groups', 'seq')), parts along dimension 0
There are 2 independent parts, one for each index of `groups`. A program takes and returns all parts, laid end to end along the dimension named above; each array names one. Nothing has to cross between parts.
Inputs may be any that keep to these rules, and one draw needn't show every extreme that they name: `block_counts`: they sum to 192; the largest equals 6. `pack_order`: each prompt number appears once. The last 1 positions hold null prompts, and the position before them a conditional prompt of 6 blocks. `decode_slot`: each slot appears once.
All inputs are finite; a program needn't handle non-finite values.
Results may differ from a plain program's by a relative error of at most 0.0034.
Values may be sent and summed in bfloat16 or wider, within the bound.
A program may use at most 64 MiB of HBM per device.

v0:
```python
import jax
import jax.numpy as jnp
from jax import lax
from jax.sharding import PartitionSpec as P

HEADS = 16
HEAD_DIM = 128
BLOCK = 128
MAXB = 6


MASKED_SCORE = -1e30


def shifted(block, axis, distance):
    devices = range(lax.axis_size(axis))
    route = [(i - distance, i) for i in devices if i - distance in devices]
    return lax.ppermute(block, axis, route)


def block_tables(block_counts, last_tokens, pack_order, decode_slot, total_blocks, block):
    pair_count = block_counts.shape[0]
    prompts = 2 * pair_count
    prompt_ids = jnp.arange(prompts, dtype=jnp.int32)
    prompt_sizes = jnp.concatenate([block_counts, jnp.ones((pair_count,), jnp.int32)])
    picked = (pack_order[:, None] == prompt_ids[None, :]).astype(jnp.int32)
    packed_sizes = jnp.sum(picked * prompt_sizes[None, :], axis=1)
    packed_tails = jnp.sum(picked * last_tokens[None, :], axis=1)
    block_ends = jnp.cumsum(packed_sizes)
    starts = block_ends - packed_sizes
    blocks = jnp.arange(total_blocks, dtype=jnp.int32)
    member = (
        (starts[None, :] <= blocks[:, None]) & (blocks[:, None] < block_ends[None, :])
    ).astype(jnp.int32)
    position = jnp.sum(member * prompt_ids[None, :], axis=1)
    prompt = jnp.sum(member * pack_order[None, :], axis=1)
    within = blocks - jnp.sum(member * starts[None, :], axis=1)
    is_last = blocks + 1 == jnp.sum(member * block_ends[None, :], axis=1)
    valid_tokens = jnp.where(is_last, jnp.sum(member * packed_tails[None, :], axis=1), block)
    pair_ids = jnp.arange(pair_count, dtype=jnp.int32)
    earlier = (decode_slot[None, :] < decode_slot[:, None]).astype(jnp.int32)
    slot_start = jnp.sum(earlier * (block_counts + 1)[None, :], axis=1)
    pair_of = prompt % pair_count
    owner = (pair_of[:, None] == pair_ids[None, :]).astype(jnp.int32)
    base_slot = jnp.sum(owner * slot_start[None, :], axis=1)
    own_count = jnp.sum(owner * block_counts[None, :], axis=1)
    destination = base_slot + jnp.where(prompt >= pair_count, own_count, within)
    hits = (destination[None, :] == blocks[:, None]).astype(jnp.int32)
    source = jnp.sum(hits * blocks[None, :], axis=1)
    return (position, valid_tokens, source)


def hand_off(paired, source, devices):
    tokens_here = paired.shape[1]
    blocks_here = tokens_here // BLOCK
    splits = devices // HEADS
    slice_len = BLOCK // splits
    outgoing = paired.reshape(2, blocks_here, splits, slice_len, HEADS, HEAD_DIM)
    outgoing = jnp.transpose(outgoing, (4, 2, 0, 1, 3, 5)).reshape(
        devices, 2, blocks_here, slice_len, HEAD_DIM
    )
    arrived = lax.all_to_all(outgoing, "seq", split_axis=0, concat_axis=2, tiled=True)
    ordered = jnp.take(arrived[0], source, axis=1)
    return (ordered[0][None], ordered[1][None])


def attend(queries, paired, position, valid_tokens, own_index, reach):
    tokens_here, features = queries.shape
    blocks_here = tokens_here // BLOCK
    pieces = [paired]
    for distance in range(1, reach + 1):
        needed = min(blocks_here, MAXB - 1 - (distance - 1) * blocks_here)
        tail_part = paired[:, tokens_here - needed * BLOCK :]
        pieces.insert(0, shifted(tail_part, "seq", distance))
    prior_count = MAXB - 1
    window = jnp.concatenate(pieces, axis=1)
    window_blocks = prior_count + blocks_here
    lead_blocks = reach * blocks_here
    padded_docs = jnp.concatenate([jnp.full((lead_blocks,), -1, jnp.int32), position])
    padded_valid = jnp.concatenate([jnp.zeros((lead_blocks,), jnp.int32), valid_tokens])
    first_block = own_index * blocks_here + lead_blocks - prior_count
    window_docs = lax.dynamic_slice_in_dim(padded_docs, first_block, window_blocks)
    window_valid = lax.dynamic_slice_in_dim(padded_valid, first_block, window_blocks)
    own_first = own_index * blocks_here
    query_docs = lax.dynamic_slice_in_dim(position, own_first, blocks_here)
    query_valid = lax.dynamic_slice_in_dim(valid_tokens, own_first, blocks_here)
    token_ids = jnp.arange(BLOCK, dtype=jnp.int32)
    key_docs = jnp.repeat(window_docs, BLOCK)
    key_limit = jnp.repeat(window_valid, BLOCK)
    key_tokens = jnp.tile(token_ids, window_blocks)
    key_order = jnp.arange(window_blocks * BLOCK, dtype=jnp.int32) - prior_count * BLOCK
    query_order = jnp.arange(tokens_here, dtype=jnp.int32)
    allowed = key_docs[None, :] == jnp.repeat(query_docs, BLOCK)[:, None]
    allowed = (
        allowed & (key_order[None, :] <= query_order[:, None]) & (key_tokens < key_limit)[None, :]
    )
    query_ok = jnp.tile(token_ids, blocks_here) < jnp.repeat(query_valid, BLOCK)
    score_scale = HEAD_DIM ** (-0.5)
    query_heads = jnp.moveaxis(queries.reshape(tokens_here, HEADS, HEAD_DIM), 1, 0)
    key_heads = jnp.moveaxis(window[0].reshape(-1, HEADS, HEAD_DIM), 1, 0)
    value_heads = jnp.moveaxis(window[1].reshape(-1, HEADS, HEAD_DIM), 1, 0)

    def one_head(operands):
        query_part, key_part, value_part = operands
        scores = (
            jnp.einsum("qd,kd->qk", query_part, key_part, preferred_element_type=jnp.float32)
            * score_scale
        )
        scores = jnp.where(allowed, scores, MASKED_SCORE)
        peak = jnp.max(scores, axis=1, keepdims=True)
        weights = jnp.exp(scores - peak)
        totals = jnp.sum(weights, axis=1, keepdims=True)
        mixed = jnp.dot(
            weights.astype(jnp.bfloat16), value_part, preferred_element_type=jnp.float32
        )
        return mixed / totals

    head_outputs = lax.map(one_head, (query_heads, key_heads, value_heads))
    merged = jnp.moveaxis(head_outputs, 0, 1).reshape(tokens_here, features)
    return jnp.where(query_ok[:, None], merged, 0.0).astype(jnp.bfloat16)


def local(queries, keys, values, block_counts, last_tokens, pack_order, decode_slot):
    devices = lax.axis_size("seq")
    own_index = lax.axis_index("seq")
    tokens_here = queries.shape[0]
    blocks_here = tokens_here // BLOCK
    reach = (MAXB + blocks_here - 2) // blocks_here
    position, valid_tokens, source = block_tables(
        block_counts, last_tokens, pack_order, decode_slot, blocks_here * devices, BLOCK
    )
    paired = jnp.stack([keys, values])
    attended = attend(queries, paired, position, valid_tokens, own_index, reach)
    cache_keys, cache_values = hand_off(paired, source, devices)
    return (attended, cache_keys, cache_values)


def solution(mesh):
    placed = (
        P(("groups", "seq"), None),
        P(("groups", "seq"), None),
        P(("groups", "seq"), None),
        P("groups"),
        P("groups"),
        P("groups"),
        P("groups"),
    )
    return jax.shard_map(
        local,
        mesh=mesh,
        in_specs=placed,
        out_specs=(
            P(("groups", "seq"), None),
            P(("groups", "seq"), None, None, None),
            P(("groups", "seq"), None, None, None),
        ),
        check_vma=False,
    )
```

profile of v0, /device:TPU:33, one launch (start us, length us, event | category | flops | bytes accessed | tf_op | source)
XLA Modules:
  0.0 243.1 jit_solution(12251069177310898664)
XLA Ops:
  0.6 1.6 copy.37
  2.8 1.5 pad_maximum_fusion
  4.3 5.6 %collective-permute-start.1 = (bf16[2,256,2048]{1,2,0:T(8,128)(2,1)}, bf16[2,256,2048]{1,2,0:T(8,128)(2,1)}, u32[]{:S(2)}, u32[]{:S(2)}) collective-permute-start(bf16[2,256,2048]{1,2,0:T(8,128)(2,1)} %pad_maximum_fusion), channel_id=1, source_target_pairs={{0,2},{1,3},{2,4},{3,5},{4,6},{5,7},{6,8},{7,9},{8,10},{9,11},{10,... | collective-permute-start | bytes 6291464 | tf_op jit(solution)/shard_map/ppermute | solution.py:18
  9.9 2.7 %collective-permute-start.2 = (bf16[2,256,2048]{1,2,0:T(8,128)(2,1)}, bf16[2,256,2048]{1,2,0:T(8,128)(2,1)}, u32[]{:S(2)}, u32[]{:S(2)}) collective-permute-start(bf16[2,256,2048]{1,2,0:T(8,128)(2,1)} %pad_maximum_fusion), channel_id=1, source_target_pairs={{0,1},{1,2},{2,3},{3,4},{4,5},{5,6},{6,7},{7,8},{8,9},{9,10},{10,1... | collective-permute-start | bytes 6291464 | tf_op jit(solution)/shard_map/ppermute | solution.py:18
  13.7 4.3 %collective-permute-start = (bf16[2,128,2048]{1,2,0:T(8,128)(2,1)}, bf16[2,128,2048]{1,2,0:T(8,128)(2,1)}, u32[]{:S(2)}, u32[]{:S(2)}) collective-permute-start(bf16[2,128,2048]{1,2,0:T(8,128)(2,1)} %fusion.20), channel_id=1, source_target_pairs={{0,3},{1,4},{2,5},{3,6},{4,7},{5,8},{6,9},{7,10},{8,11},{9,12},{10... | collective-permute-start | bytes 3145736 | tf_op jit(solution)/shard_map/ppermute | solution.py:18
  18.7 1.9 copy.43
  20.6 28.4 %all-to-all-start = ((bf16[128,2,2,16,128]{4,3,2,1,0:T(8,128)(2,1)}), bf16[128,2,2,16,128]{4,3,2,1,0:T(8,128)(2,1)}, u32[]{:S(2)}, u32[]{:S(2)}) async-start(bf16[128,2,2,16,128]{4,3,2,1,0:T(8,128)(2,1)} %bitcast.84), calls=%async_computation | async-start | bytes 4194304 | tf_op jit(solution)/shard_map/all_to_all | solution.py:62
  50.7 2.3 copy.36
  53.2 62.3 %collective-permute-done = bf16[2,128,2048]{1,2,0:T(8,128)(2,1)} collective-permute-done((bf16[2,128,2048]{1,2,0:T(8,128)(2,1)}, bf16[2,128,2048]{1,2,0:T(8,128)(2,1)}, u32[]{:S(2)}, u32[]{:S(2)}) %collective-permute-start) | collective-permute-done | bytes 1048608 | tf_op jit(solution)/shard_map/ppermute | solution.py:18
  115.5 3.5 %maximum_maximum_fusion = bf16[2,896,2048]{1,2,0:T(8,128)(2,1)S(1)} fusion(bf16[1,256,2048]{1,2,0:T(8,128)(2,1)S(1)} %bitcast.82, bf16[1,256,2048]{1,2,0:T(8,128)(2,1)S(1)} %bitcast.79, bf16[2,256,2048]{1,2,0:T(8,128)(2,1)} %collective-permute-done.2, bf16[2,256,2048]{1,2,0:T(8,128)(2,1)} %collective-permute-done.1, ...), kind=kLoop, calls=%fused_computation.22 | loop fusion | flops 36700160 | bytes 14680064 | tf_op jit(solution)/shard_map/concatenate | solution.py:76
  119.0 3.6 %fusion.26 = (bf16[1,896,2048]{1,2,0:T(8,128)(2,1)}, bf16[1,896,2048]{1,2,0:T(8,128)(2,1)}) fusion(bf16[2,896,2048]{1,2,0:T(8,128)(2,1)S(1)} %maximum_maximum_fusion), kind=kLoop, calls=%fused_computation.71 | loop fusion | bytes 14680064 | tf_op jit(solution)/shard_map/slice | solution.py:101
  122.6 50.8 %while.11 = (s32[]{:T(128)}, bf16[16,256,128]{2,1,0:T(8,128)(2,1)S(1)}, bf16[16,256,128]{1,2,0:T(8,128)(2,1)}, bf16[16,896,128]{1,2,0:T(8,128)(2,1)}, bf16[16,89...) while((s32[]{:T(128)}, ...), condition=%wide.region_9.10_spmd.clone, body=%wide.region_6.0_spmd.clone.sunk | while | flops 119995904 | bytes 3424229 | solution.py:118
  122.6 1.5 fusion.35
  124.4 1.3 fusion.37
  125.7 1.5 fusion.35
  127.6 1.3 fusion.37
  128.9 1.5 fusion.35
  130.8 1.3 fusion.37
  132.1 1.5 fusion.35
  133.9 1.3 fusion.37
  135.3 1.5 fusion.35
  137.1 1.3 fusion.37
  138.5 1.5 fusion.35
  140.3 1.3 fusion.37
  141.6 1.5 fusion.35
  143.5 1.3 fusion.37
  144.8 1.5 fusion.35
  146.6 1.3 fusion.37
  148.0 1.5 fusion.35
  149.8 1.3 fusion.37
  151.2 1.5 fusion.35
  153.0 1.3 fusion.37
  154.3 1.5 fusion.35
  156.2 1.3 fusion.37
  157.5 1.5 fusion.35
  159.3 1.3 fusion.37
  160.7 1.5 fusion.35
  162.5 1.3 fusion.37
  163.9 1.5 fusion.35
  165.7 1.3 fusion.37
  167.0 1.5 fusion.35
  168.9 1.3 fusion.37
  170.2 1.5 fusion.35
  172.0 1.3 fusion.37
  174.6 59.9 %all-to-all-done = bf16[128,2,2,16,128]{4,3,2,1,0:T(8,128)(2,1)} async-done(((bf16[128,2,2,16,128]{4,3,2,1,0:T(8,128)(2,1)}), bf16[128,2,2,16,128]{4,3,2,1,0:T(8,128)(2,1)}, u32[]{:S(2)}, u32[]{:S(2)}) %all-to-all-start) | async-done | bytes 2097184 | tf_op jit(solution)/shard_map/all_to_all | solution.py:62
  234.5 3.3 %copy.44 = bf16[1,2,128,2,16,128]{5,4,3,2,1,0:T(8,128)(2,1)} copy(bf16[1,2,128,2,16,128]{5,4,3,1,2,0:T(8,128)(2,1)} %bitcast.17) | data formatting | bytes 4194304 | tf_op jit(solution)/shard_map/all_to_all | solution.py:62
  237.8 2.7 %gather_fusion = bf16[256,2,16,128]{3,2,1,0:T(8,128)(2,1)S(1)} fusion(bf16[2,256,16,128]{3,2,1,0:T(8,128)(2,1)} %bitcast.83, s32[1024]{0:T(1024)S(1)} %pad_clamp_fusion), kind=kCustom, calls=%fused_computation | custom fusion | bytes 4195328 | tf_op jit(solution)/shard_map/jit(_take)/gather | solution.py:63
  241.4 1.7 slice_bitcast_fusion
  (63 shorter events, 11.1 us)
Async XLA Ops:
  0.6 1.6 copy-start.1
  4.3 13.7 %copy-start = (bf16[256,2048]{1,0:T(8,128)(2,1)S(1)}, bf16[256,2048]{1,0:T(8,128)(2,1)}, u32[]{:S(2)}) copy-start(bf16[256,2048]{1,0:T(8,128)(2,1)} %param.10) | copy-start | bytes 3145732
  4.3 111.2 %collective-permute-start.1 = (bf16[2,256,2048]{1,2,0:T(8,128)(2,1)}, bf16[2,256,2048]{1,2,0:T(8,128)(2,1)}, u32[]{:S(2)}, u32[]{:S(2)}) collective-permute-start(bf16[2,256,2048]{1,2,0:T(8,128)(2,1)} %pad_maximum_fusion), channel_id=1, source_target_pairs={{0,2},{1,3},{2,4},{3,5},{4,6},{5,7},{6,8},{7,9},{8,10},{9,11},{10,... | collective-permute-start | bytes 6291464 | tf_op jit(solution)/shard_map/ppermute | solution.py:18
  9.9 105.7 %collective-permute-start.2 = (bf16[2,256,2048]{1,2,0:T(8,128)(2,1)}, bf16[2,256,2048]{1,2,0:T(8,128)(2,1)}, u32[]{:S(2)}, u32[]{:S(2)}) collective-permute-start(bf16[2,256,2048]{1,2,0:T(8,128)(2,1)} %pad_maximum_fusion), channel_id=1, source_target_pairs={{0,1},{1,2},{2,3},{3,4},{4,5},{5,6},{6,7},{7,8},{8,9},{9,10},{10,1... | collective-permute-start | bytes 6291464 | tf_op jit(solution)/shard_map/ppermute | solution.py:18
  13.7 101.8 %collective-permute-start = (bf16[2,128,2048]{1,2,0:T(8,128)(2,1)}, bf16[2,128,2048]{1,2,0:T(8,128)(2,1)}, u32[]{:S(2)}, u32[]{:S(2)}) collective-permute-start(bf16[2,128,2048]{1,2,0:T(8,128)(2,1)} %fusion.20), channel_id=1, source_target_pairs={{0,3},{1,4},{2,5},{3,6},{4,7},{5,8},{6,9},{7,10},{8,11},{9,12},{10... | collective-permute-start | bytes 3145736 | tf_op jit(solution)/shard_map/ppermute | solution.py:18
  20.6 28.4 %copy-start.5 = (s32[64]{0:T(128)S(1)}, s32[64]{0:T(128)}, u32[]{:S(2)}) copy-start(s32[64]{0:T(128)} %param.12) | copy-start | bytes 772
  20.6 28.4 %copy-start.2 = (s32[128]{0:T(128)S(1)}, s32[128]{0:T(128)}, u32[]{:S(2)}) copy-start(s32[128]{0:T(128)} %param.14) | copy-start | bytes 1540
  20.6 28.4 %copy-start.4 = (s32[128]{0:T(128)S(1)}, s32[128]{0:T(128)}, u32[]{:S(2)}) copy-start(s32[128]{0:T(128)} %param.13) | copy-start | bytes 1540
  20.6 29.4 %copy-start.3 = (s32[64]{0:T(128)S(1)}, s32[64]{0:T(128)}, u32[]{:S(2)}) copy-start(s32[64]{0:T(128)} %param.15) | copy-start | bytes 772
  20.6 213.9 %all-to-all-start = ((bf16[128,2,2,16,128]{4,3,2,1,0:T(8,128)(2,1)}), bf16[128,2,2,16,128]{4,3,2,1,0:T(8,128)(2,1)}, u32[]{:S(2)}, u32[]{:S(2)}) async-start(bf16[128,2,2,16,128]{4,3,2,1,0:T(8,128)(2,1)} %bitcast.84), calls=%async_computation | async-start | bytes 4194304 | tf_op jit(solution)/shard_map/all_to_all | solution.py:62
where the time goes:
time: 244 us; the launch traced here: 243 us
  waiting for transfers between devices  122 us (50%)
  matrix products  45.6 us (19%)
  starting transfers between devices  41 us (17%)
  local copies, waits for them, and re-layouts  18.5 us (8%)
  other arithmetic  14.6 us (6%)
    ppermute x3, waiting for transfers between devices, shifted(): return lax.ppermute(block, axis, route)  62.3 us
    all_to_all x1, waiting for transfers between devices, hand_off(): lax.all_to_all(outgoing, 'seq', split_axis=0, concat_axis=2, tiled=True)  59.9 us
    all_to_all x1, starting transfers between devices, hand_off(): lax.all_to_all(outgoing, 'seq', split_axis=0, concat_axis=2, tiled=True)  28.4 us
    dot_general x16, matrix products, one_head(): jnp.einsum('qd,kd->qk', query_part, key_part, preferred_element_type=jnp....  24.4 us
    dot_general x16, matrix products, one_head(): jnp.dot(weights.astype(jnp.bfloat16), value_part, preferred_element_type=...  21.2 us
    ppermute x3, starting transfers between devices, shifted(): return lax.ppermute(block, axis, route)  12.6 us
    unnamed x18, local copies, waits for them, and re-layouts  6.51 us
  transfers between devices with their start and end apart: 4, of which 2 were waited for; matrix products, arithmetic and copies ran while one was open for 27% of the time, Pallas kernels for 0%

commit v1 on v0

v1 whole, which is shorter than its diff:
```python
import functools

import jax
import jax.numpy as jnp
from jax import lax
from jax.experimental import pallas as pl
from jax.experimental.pallas import tpu as pltpu
from jax.sharding import PartitionSpec as P

HEADS = 16
HEAD_DIM = 128
BLOCK = 128
MAXB = 6
PRIOR = MAXB - 1
MASKED_SCORE = -1e30
MESH = pl.DeviceIdType.MESH
BF16 = jnp.bfloat16
F32 = jnp.float32


def column(row):
    n = row.shape[1]
    diagonal = lax.broadcasted_iota(jnp.int32, (n, n), 0) == lax.broadcasted_iota(jnp.int32, (n, n), 1)
    return jnp.sum(jnp.where(diagonal, row, 0), axis=1, keepdims=True)


def pick(mask, values):
    return jnp.sum(jnp.where(mask, values, 0), axis=0, keepdims=True)


def block_tables(counts_ref, tails_ref, order_ref, slots_ref, rows_ref, table_ref):
    pairs = counts_ref.shape[1]
    prompts = order_ref.shape[1]
    blocks = table_ref.shape[1]

    def iota(shape, axis):
        return lax.broadcasted_iota(jnp.int32, shape, axis)

    rows_ref[0:1, :] = jnp.zeros((1, prompts), jnp.int32)
    rows_ref[1:2, :] = jnp.ones((1, prompts), jnp.int32)
    rows_ref[2:3, :] = jnp.full((1, prompts), 1 << 20, jnp.int32)
    rows_ref[0:1, 0:pairs] = counts_ref[...]
    rows_ref[1:2, 0:pairs] = counts_ref[...]
    rows_ref[2:3, 0:pairs] = slots_ref[...]
    counts = rows_ref[0:1, :]
    sizes = rows_ref[1:2, :]
    slots = rows_ref[2:3, :]
    order = order_ref[...]
    tails = tails_ref[...]

    square = (prompts, prompts)
    picked = iota(square, 0) == order
    packed_sizes = pick(picked, column(sizes))
    packed_tails = pick(picked, column(tails))
    ends = pick(iota(square, 0) <= iota(square, 1), column(packed_sizes))
    starts = ends - packed_sizes

    wide = (prompts, blocks)
    block = iota((1, blocks), 1)
    ends_column = column(ends)
    starts_column = column(starts)
    member = (starts_column <= block) & (block < ends_column)
    position = pick(member, iota(wide, 0))
    prompt = pick(member, column(order))
    within = block - pick(member, starts_column)
    last = block + 1 == pick(member, ends_column)
    valid = jnp.where(last, pick(member, column(packed_tails)), BLOCK)

    slot_start = pick(column(slots) < slots, column(counts) + 1)
    null = prompt >= pairs
    owner = iota(wide, 0) == jnp.where(null, prompt - pairs, prompt)
    destination = pick(owner, column(slot_start)) + jnp.where(null, pick(owner, column(counts)), within)
    full = (blocks, blocks)
    source = jnp.minimum(pick(column(destination) == iota(full, 1), iota(full, 0)), blocks - 1)

    table_ref[0:1, :] = position
    table_ref[1:2, :] = valid
    table_ref[2:3, :] = source


def exchange_kernel(
    rows,
    cols,
    q_ref,
    k_ref,
    v_ref,
    counts_ref,
    tails_ref,
    order_ref,
    slots_ref,
    att_ref,
    out_k,
    out_v,
    win,
    q_vmem,
    stage,
    cross,
    recv,
    allowed,
    small_rows,
    table_vmem,
    table,
    load_sem,
    table_sem,
    halo_sem,
    halo_send,
    cross_sem,
    cross_send,
    relay_send,
    z_send,
    z_sem,
    row_send,
    row_sem,
    lower_ready,
    upper_ready,
):
    me = lax.axis_index("seq")
    z = me // cols
    i = lax.rem(me, cols)
    x = i // 2
    core = lax.rem(i, 2)
    own = PRIOR
    here = win.shape[1] - PRIOR
    group = win.shape[3] // (cols // 2)
    part = BLOCK // cols

    def device(row, place):
        return {"seq": row * cols + place}

    def send(src, dst, ssem, rsem, target):
        return pltpu.make_async_remote_copy(
            src_ref=src, dst_ref=dst, send_sem=ssem, recv_sem=rsem, device_id=target, device_id_type=MESH
        )

    loads = [
        pltpu.make_async_copy(k_ref, win.at[0, pl.ds(own, here)], load_sem.at[0]),
        pltpu.make_async_copy(v_ref, win.at[1, pl.ds(own, here)], load_sem.at[1]),
        pltpu.make_async_copy(q_ref, q_vmem, load_sem.at[2]),
    ]
    for load in loads:
        load.start()

    barrier = pltpu.get_barrier_semaphore()

    def greet_row(row, first):
        def greet(k, carry):
            place = lax.rem(i + k, cols)
            pl.semaphore_signal(barrier, inc=1, device_id=device(row, place), device_id_type=MESH)
            return carry

        lax.fori_loop(first, cols, greet, 0)

    greet_row(z, 1)

    @pl.when(z > 0)
    def _():
        greet_row(z - 1, 0)

    @pl.when(z < rows - 1)
    def _():
        greet_row(z + 1, 0)

    for load in loads:
        load.wait()
    next_rows = jnp.where(z > 0, cols, 0) + jnp.where(z < rows - 1, cols, 0)
    pl.semaphore_wait(barrier, cols - 1 + next_rows)

    spans = {cols - 1: (PRIOR - 2, 2), cols - 2: (PRIOR - 4, 2), cols - 3: (0, 1)}
    has_next = z < rows - 1

    def columns_of(g):
        return pl.ds(pl.multiple_of(g * group, group), group)

    def crossing(place, g):
        first, length = spans[place]
        n = place - (cols - 3)
        src = win.at[:, pl.ds(own + here - length, length), :, columns_of(g)]
        if place // 2 == g:
            return send(
                src,
                win.at[:, pl.ds(first, length), :, columns_of(g)],
                cross_send.at[n, g],
                halo_sem.at[0 if place == cols - 1 else 1],
                device(z + 1, 0),
            )
        return send(
            src, cross.at[:, pl.ds(first, length)], cross_send.at[n, g], cross_sem.at[n], device(z, 2 * g + 1)
        )

    for place in spans:

        @pl.when(has_next & (i == place))
        def _(place=place):
            for g in range(cols // 2):
                crossing(place, g).start()

    def next_odd():
        return send(
            win.at[:, pl.ds(own, here)],
            win.at[:, pl.ds(PRIOR - here, here)],
            halo_send.at[0],
            halo_sem.at[0],
            device(z, i + 1),
        )

    def next_even():
        return send(
            win.at[:, pl.ds(own, here)],
            win.at[:, pl.ds(PRIOR - 2 * here, here)],
            halo_send.at[1],
            halo_sem.at[1],
            device(z, i + 2),
        )

    def pass_last():
        return send(
            win.at[:, pl.ds(PRIOR - 1, 1)],
            win.at[:, pl.ds(0, 1)],
            halo_send.at[2],
            halo_sem.at[1],
            device(z, i + 2),
        )

    def pass_pair():
        return send(
            win.at[:, pl.ds(PRIOR - here, here)],
            win.at[:, pl.ds(PRIOR - 2 * here, here)],
            halo_send.at[3],
            halo_sem.at[1],
            device(z, i + 1),
        )

    def pass_single():
        return send(
            win.at[:, pl.ds(PRIOR - here - 1, 1)],
            win.at[:, pl.ds(0, 1)],
            halo_send.at[4],
            halo_sem.at[1],
            device(z, i + 1),
        )

    even = core == 0
    has_two_on = even & (i < cols - 2)

    @pl.when(i < cols - 1)
    def _():
        next_odd().start()

    @pl.when(has_two_on)
    def _():
        next_even().start()

    @pl.when(me == 0)
    def _():
        for n, ref in enumerate((k_ref, v_ref)):
            pltpu.make_async_copy(ref, win.at[n, pl.ds(PRIOR - here, here)], halo_sem.at[0]).start()
            pltpu.make_async_copy(ref, win.at[n, pl.ds(PRIOR - 2 * here, here)], halo_sem.at[1]).start()
            pltpu.make_async_copy(ref.at[pl.ds(0, 1)], win.at[n, pl.ds(0, 1)], halo_sem.at[1]).start()

    def head_columns(row):
        return pl.ds(pl.multiple_of(row * HEAD_DIM, HEAD_DIM), HEAD_DIM)

    def slice_of(place):
        return pl.ds(pl.multiple_of(place * part, part), part)

    def blocks_of(row):
        return pl.ds((row * cols + i) * here, here)

    def give_own(k, carry):
        place = lax.rem(i + k, cols)
        send(
            win.at[:, pl.ds(own, here), slice_of(place), head_columns(z)],
            recv.at[:, blocks_of(z)],
            row_send,
            row_sem,
            device(z, place),
        ).start()
        return carry

    lax.fori_loop(1, cols, give_own, 0)
    recv[:, blocks_of(z)] = win[:, own : own + here, slice_of(i), head_columns(z)]

    @pl.when(z > 0)
    def _():
        pl.semaphore_wait(lower_ready, 1)

    @pl.when(z < rows - 1)
    def _():
        pl.semaphore_signal(lower_ready, inc=1, device_id=device(z + 1, i), device_id_type=MESH)

    def tell(row, carry):
        pl.semaphore_signal(upper_ready.at[z], inc=1, device_id=device(row, i), device_id_type=MESH)
        return carry

    lax.fori_loop(0, z, tell, 0)

    def give_head(row):
        send(
            win.at[:, pl.ds(own, here), :, head_columns(row)],
            stage.at[z],
            z_send,
            z_sem.at[z],
            device(row, i),
        ).start()

    def give_below(k, carry):
        give_head(z - k)
        return carry

    half = rows // 2
    near = jnp.minimum(z, half)
    lax.fori_loop(1, near + 1, give_below, 0)

    def relay(place):
        first, length = spans[place]
        return send(
            cross.at[:, pl.ds(first, length)],
            win.at[:, pl.ds(first, length), :, columns_of(x)],
            relay_send.at[place - (cols - 3)],
            halo_sem.at[0 if place == cols - 1 else 1],
            device(z + 1, 0),
        )

    for place in spans:

        @pl.when(has_next & (core == 1) & (x != place // 2))
        def _(place=place):
            first, length = spans[place]
            span = cross.at[:, pl.ds(first, length)]
            pltpu.make_async_copy(span, span, cross_sem.at[place - (cols - 3)]).wait()
            relay(place).start()

    lax.fori_loop(near + 1, z + 1, give_below, 0)

    def give_above(row, carry):
        pl.semaphore_wait(upper_ready.at[row], 1)
        give_head(row)
        return carry

    lax.fori_loop(z + 1, rows, give_above, 0)

    block_tables(counts_ref, tails_ref, order_ref, slots_ref, small_rows, table_vmem)

    def arrived(step):
        k = step // 2 + 1
        row = lax.rem(z + jnp.where(lax.rem(step, 2) == 0, k, rows - k), rows)
        pltpu.make_async_copy(stage.at[row], stage.at[row], z_sem.at[row]).wait()

        def give(n, carry):
            place = lax.rem(i + n, cols)
            send(
                stage.at[row, :, :, slice_of(place), :],
                recv.at[:, blocks_of(row)],
                row_send,
                row_sem,
                device(z, place),
            ).start()
            return carry

        lax.fori_loop(1, cols, give, 0)
        recv[:, blocks_of(row)] = stage[row, :, :, slice_of(i), :]

    early = (rows - 1) // 2

    def early_step(step, carry):
        arrived(step)
        return carry

    lax.fori_loop(0, early, early_step, 0)

    table_copy = pltpu.make_async_copy(table_vmem, table, table_sem)
    table_copy.start()
    table_copy.wait()

    late_half = win.at[:, pl.ds(PRIOR - here, here)]
    pltpu.make_async_copy(late_half, late_half, halo_sem.at[0]).wait()

    @pl.when(has_two_on)
    def _():
        pass_last().start()

    @pl.when(even)
    def _():
        pass_pair().start()

    early_half = win.at[:, pl.ds(0, PRIOR - here)]
    pltpu.make_async_copy(early_half, early_half, halo_sem.at[1]).wait()

    @pl.when(even)
    def _():
        pass_single().start()

    tokens = here * BLOCK
    span = MAXB * BLOCK - BLOCK + tokens
    query = lax.broadcasted_iota(jnp.int32, (tokens, BLOCK), 0)
    query_block = query // BLOCK
    token = lax.broadcasted_iota(jnp.int32, (tokens, BLOCK), 1)
    first_block = me * here
    query_doc = jnp.zeros((tokens, BLOCK), jnp.int32)
    query_valid = jnp.zeros((tokens, BLOCK), jnp.int32)
    for b in range(here):
        query_doc = jnp.where(query_block == b, table[0, first_block + b], query_doc)
        query_valid = jnp.where(query_block == b, table[1, first_block + b], query_valid)
    query_ok = lax.rem(query, BLOCK) < query_valid
    for b in range(PRIOR + here):
        block = first_block + b - PRIOR
        there = jnp.maximum(block, 0)
        doc = jnp.where(block >= 0, table[0, there], -1)
        limit = jnp.where(block >= 0, table[1, there], 0)
        seen = (query_doc == doc) & (token < limit) & (token + (b - PRIOR) * BLOCK <= query)
        allowed[:, b * BLOCK : (b + 1) * BLOCK] = seen.astype(F32)

    def attend(head):
        at = head_columns(head)
        keys = win[0, :, :, at].reshape(span, HEAD_DIM)
        values = win[1, :, :, at].reshape(span, HEAD_DIM)
        scores = lax.dot_general(
            q_vmem[:, at], keys, (((1,), (1,)), ((), ())), preferred_element_type=F32
        ) * (HEAD_DIM**-0.5)
        scores = jnp.where(allowed[...] > 0.5, scores, MASKED_SCORE)
        peak = jnp.max(scores, axis=1, keepdims=True)
        weights = jnp.exp(scores - peak)
        totals = jnp.sum(weights, axis=1, keepdims=True)
        mixed = jnp.dot(weights.astype(BF16), values, preferred_element_type=F32)
        att_ref[:, at] = jnp.where(query_ok, mixed / totals, 0.0).astype(BF16)

    per_step = HEADS // (rows - 1 - early)

    def late_step(step, carry):
        def one(n, c):
            attend((step - early) * per_step + n)
            return c

        lax.fori_loop(0, per_step, one, 0)
        arrived(step)
        return carry

    lax.fori_loop(early, rows - 1, late_step, 0)

    def rest(head, carry):
        attend(head)
        return carry

    lax.fori_loop(per_step * (rows - 1 - early), HEADS, rest, 0)

    landed = recv.at[:, pl.ds(0, rows * (cols - 1) * here)]
    pltpu.make_async_copy(landed, landed, row_sem).wait()

    def place_block(c, carry):
        s = jnp.clip(table[2, c], 0, out_k.shape[0] - 1)
        out_k[c] = recv[0, s]
        out_v[c] = recv[1, s]
        return carry

    lax.fori_loop(0, out_k.shape[0], place_block, 0, unroll=8)

    pltpu.make_async_copy(landed, landed, row_send).wait()
    heads_sent = stage.at[pl.ds(0, rows - 1)]
    pltpu.make_async_copy(heads_sent, heads_sent, z_send).wait()
    for place in spans:

        @pl.when(has_next & (i == place))
        def _(place=place):
            for g in range(cols // 2):
                crossing(place, g).wait_send()

        @pl.when(has_next & (core == 1) & (x != place // 2))
        def _(place=place):
            relay(place).wait_send()

    @pl.when(i < cols - 1)
    def _():
        next_odd().wait_send()

    @pl.when(has_two_on)
    def _():
        next_even().wait_send()
        pass_last().wait_send()

    @pl.when(even)
    def _():
        pass_pair().wait_send()
        pass_single().wait_send()


def local(queries, keys, values, block_counts, last_tokens, pack_order, decode_slot):
    devices = lax.axis_size("seq")
    tokens, features = queries.shape
    here = tokens // BLOCK
    cols = devices // HEADS
    rows = HEADS
    blocks = devices * here
    part = BLOCK // cols
    prompts = pack_order.shape[0]
    window = PRIOR + here
    hbm = pl.BlockSpec(memory_space=pltpu.HBM)
    vmem = pl.BlockSpec(memory_space=pltpu.VMEM)
    dma = pltpu.SemaphoreType.DMA
    regular = pltpu.SemaphoreType.REGULAR
    shapes = ((tokens, features), (blocks, part, HEAD_DIM), (blocks, part, HEAD_DIM))
    attended, cache_keys, cache_values = pl.pallas_call(
        functools.partial(exchange_kernel, rows, cols),
        out_shape=[pltpu.VMEM(shape, BF16) for shape in shapes],
        in_specs=[hbm] * 3 + [vmem] * 4,
        out_specs=[vmem] * 3,
        scratch_shapes=[
            pltpu.VMEM((2, window, BLOCK, features), BF16),
            pltpu.VMEM((tokens, features), BF16),
            pltpu.VMEM((rows, 2, here, BLOCK, HEAD_DIM), BF16),
            pltpu.VMEM((2, PRIOR, BLOCK, features // (cols // 2)), BF16),
            pltpu.VMEM((2, blocks, part, HEAD_DIM), BF16),
            pltpu.VMEM((tokens, window * BLOCK), F32),
            pltpu.VMEM((8, prompts), jnp.int32),
            pltpu.VMEM((8, blocks), jnp.int32),
            pltpu.SMEM((8, blocks), jnp.int32),
            dma((3,)),
            dma,
            dma((2,)),
            dma((5,)),
            dma((3,)),
            dma((3, cols // 2)),
            dma((3,)),
            dma,
            dma((rows,)),
            dma,
            dma,
            regular,
            regular((rows,)),
        ],
        compiler_params=pltpu.CompilerParams(
            collective_id=0, has_side_effects=True, vmem_limit_bytes=60 * 1024 * 1024
        ),
    )(
        queries,
        keys.reshape(here, BLOCK, features),
        values.reshape(here, BLOCK, features),
        block_counts.reshape(1, -1),
        last_tokens.reshape(1, -1),
        pack_order.reshape(1, -1),
        decode_slot.reshape(1, -1),
    )
    return (attended, cache_keys[None], cache_values[None])


def solution(mesh):
    placed = (P(("groups", "seq"), None),) * 3 + (P("groups"),) * 4
    return jax.shard_map(
        local,
        mesh=mesh,
        in_specs=placed,
        out_specs=(
            P(("groups", "seq"), None),
            P(("groups", "seq"), None, None, None),
            P(("groups", "seq"), None, None, None),
        ),
        check_vma=False,
    )
```

time: 244 us -> 161 us (0.66)
  Pallas kernels: 0 us -> 156 us
  waiting for transfers between devices: 122 us -> 0 us
  matrix products: 45.6 us -> 0 us
  starting transfers between devices: 41 us -> 0 us
  local copies, waits for them, and re-layouts: 18.5 us -> 2.91 us
  other arithmetic: 14.6 us -> 0 us
    pallas_call x0 -> x1, Pallas kernels: none -> 156 us  [local(): pl.pallas_call(functools.partial(exchange_kernel, rows, cols), out_shape=...]
    ppermute x3 -> x0, waiting for transfers between devices: 62.3 us -> none  [shifted(): return lax.ppermute(block, axis, route)]
    all_to_all x1 -> x0, waiting for transfers between devices: 59.9 us -> none  [hand_off(): lax.all_to_all(outgoing, 'seq', split_axis=0, concat_axis=2, tiled=True)]
    dot_general x32 -> x0, matrix products: 45.6 us -> none  [the longest x16 24.4 us: one_head(): jnp.einsum('qd,kd->qk', query_part, key_part, preferred_element_type=jnp....]
    all_to_all x1 -> x0, starting transfers between devices: 28.4 us -> none  [hand_off(): lax.all_to_all(outgoing, 'seq', split_axis=0, concat_axis=2, tiled=True)]
    ppermute x3 -> x0, starting transfers between devices: 12.6 us -> none  [shifted(): return lax.ppermute(block, axis, route)]
    reduce_sum x21 -> x0, other arithmetic: 5.62 us -> none  [the longest x16 4.8 us: one_head(): totals = jnp.sum(weights, axis=1, keepdims=True)]
    unnamed x18 -> x3, local copies, waits for them, and re-layouts: 6.51 us -> 2.91 us
  transfers between devices with their start and end apart: 4 -> 0, of which waited for: 2 -> 0; matrix products, arithmetic and copies ran while one was open for 27% -> 0% of each run, Pallas kernels for 0% -> 0%
where the time goes in v1:
time: 161 us; the launch traced here: 160 us
  Pallas kernels  156 us (97%)
  local copies, waits for them, and re-layouts  2.91 us (2%)
    pallas_call x1, Pallas kernels, local(): pl.pallas_call(functools.partial(exchange_kernel, rows, cols), out_shape=...  156 us

profile of v1, /device:TPU:33, one launch (start us, length us, event | category | flops | bytes accessed | tf_op | source)
XLA Modules:
  0.0 159.6 jit_solution(10790577317346416736)
XLA Ops:
  0.6 156.1 %shard_map.94 = (bf16[256,2048]{1,0:T(8,128)(2,1)S(1)}, bf16[256,16,128]{2,1,0:T(8,128)(2,1)S(1)}, bf16[256,16,128]{2,1,0:T(8,128)(2,1)S(1)}) custom-call(bf16[256,2048]{1,0:T(8,128)(2,1)} %q_ref.1, bf16[2,128,2048]{2,1,0:T(8,128)(2,1)} %bitcast.10, bf16[2,128,2048]{2,1,0:T(8,128)(2,1)} %bitcast.11, s32[1,64]{1,0:T(1,128)} %bitcast.12, s32[1,128]{1,0:T(1,128)} %bitcast.13, ...), custom_call_target="tpu_custom_call" | custom-call | tf_op jit(solution)/shard_map/pallas_call | solution.py:501
  156.7 1.0 copy.13
  157.7 1.0 copy.14
  158.6 1.0 copy.15

commit v2 on v1

--- a/solution.py
+++ b/solution.py
@@ -93,10 +93,13 @@
     out_v,
     win,
     q_vmem,
-    stage,
     cross,
     recv,
     allowed,
+    counts,
+    tails,
+    order,
+    slots,
     small_rows,
     table_vmem,
     table,
@@ -107,8 +110,6 @@
     cross_sem,
     cross_send,
     relay_send,
-    z_send,
-    z_sem,
     row_send,
     row_sem,
     lower_ready,
@@ -135,39 +136,69 @@
     loads = [
         pltpu.make_async_copy(k_ref, win.at[0, pl.ds(own, here)], load_sem.at[0]),
         pltpu.make_async_copy(v_ref, win.at[1, pl.ds(own, here)], load_sem.at[1]),
-        pltpu.make_async_copy(q_ref, q_vmem, load_sem.at[2]),
     ]
-    for load in loads:
+    later = [
+        pltpu.make_async_copy(src, dst, load_sem.at[2 + n])
+        for n, (src, dst) in enumerate(
+            (
+                (q_ref, q_vmem),
+                (counts_ref, counts),
+                (tails_ref, tails),
+                (order_ref, order),
+                (slots_ref, slots),
+            )
+        )
+    ]
+
+    barrier = pltpu.get_barrier_semaphore()
+
+    def greet(row, place):
+        pl.semaphore_signal(barrier, inc=1, device_id=device(row, place), device_id_type=MESH)
+
+    def greet_row(k, carry):
+        greet(z, lax.rem(i + k, cols))
+        return carry
+
+    lax.fori_loop(1, cols, greet_row, 0)
+    line = lax.rem(z + rows - 1, rows)
+    line_first, line_last = line == 0, line == rows - 1
+
+    def row_at(place):
+        return lax.rem(place + 1, rows)
+
+    @pl.when(jnp.logical_not(line_first))
+    def _():
+        greet(row_at(line - 1), i)
+
+    @pl.when(jnp.logical_not(line_last))
+    def _():
+        greet(row_at(line + 1), i)
+
+    has_next = z < rows - 1
+    senders = [place for place in range(cols) if place % 2 == 1 or place >= cols - 3]
+    crosses = core == 1
+    for place in senders:
+        crosses = crosses | (i == place)
+    crosses = crosses & has_next
+    receives = (i == 0) & (z > 0)
+
+    @pl.when(crosses)
+    def _():
+        greet(z + 1, 0)
+
+    @pl.when(receives)
+    def _():
+        for place in senders:
+            greet(z - 1, place)
+
+    for load in loads + later:
         load.start()
-
-    barrier = pltpu.get_barrier_semaphore()
-
-    def greet_row(row, first):
-        def greet(k, carry):
-            place = lax.rem(i + k, cols)
-            pl.semaphore_signal(barrier, inc=1, device_id=device(row, place), device_id_type=MESH)
-            return carry
-
-        lax.fori_loop(first, cols, greet, 0)
-
-    greet_row(z, 1)
-
-    @pl.when(z > 0)
-    def _():
-        greet_row(z - 1, 0)
-
-    @pl.when(z < rows - 1)
-    def _():
-        greet_row(z + 1, 0)
-
+    peers = cols - 1 + jnp.where(line_first, 0, 1) + jnp.where(line_last, 0, 1)
+    pl.semaphore_wait(barrier, peers + jnp.where(crosses, 1, 0) + jnp.where(receives, len(senders), 0))
     for load in loads:
         load.wait()
-    next_rows = jnp.where(z > 0, cols, 0) + jnp.where(z < rows - 1, cols, 0)
-    pl.semaphore_wait(barrier, cols - 1 + next_rows)
 
     spans = {cols - 1: (PRIOR - 2, 2), cols - 2: (PRIOR - 4, 2), cols - 3: (0, 1)}
-    has_next = z < rows - 1
-
     def columns_of(g):
         return pl.ds(pl.multiple_of(g * group, group), group)
 
@@ -263,14 +294,13 @@
     def slice_of(place):
         return pl.ds(pl.multiple_of(place * part, part), part)
 
-    def blocks_of(row):
-        return pl.ds((row * cols + i) * here, here)
+    mine = pl.ds(me * here, here)
 
     def give_own(k, carry):
         place = lax.rem(i + k, cols)
         send(
             win.at[:, pl.ds(own, here), slice_of(place), head_columns(z)],
-            recv.at[:, blocks_of(z)],
+            recv.at[:, mine],
             row_send,
             row_sem,
             device(z, place),
@@ -278,38 +308,49 @@
         return carry
 
     lax.fori_loop(1, cols, give_own, 0)
-    recv[:, blocks_of(z)] = win[:, own : own + here, slice_of(i), head_columns(z)]
-
-    @pl.when(z > 0)
+    recv[:, mine] = win[:, own : own + here, slice_of(i), head_columns(z)]
+
+    @pl.when(jnp.logical_not(line_first))
     def _():
         pl.semaphore_wait(lower_ready, 1)
 
-    @pl.when(z < rows - 1)
-    def _():
-        pl.semaphore_signal(lower_ready, inc=1, device_id=device(z + 1, i), device_id_type=MESH)
-
-    def tell(row, carry):
-        pl.semaphore_signal(upper_ready.at[z], inc=1, device_id=device(row, i), device_id_type=MESH)
-        return carry
-
-    lax.fori_loop(0, z, tell, 0)
-
-    def give_head(row):
-        send(
-            win.at[:, pl.ds(own, here), :, head_columns(row)],
-            stage.at[z],
-            z_send,
-            z_sem.at[z],
-            device(row, i),
-        ).start()
+    @pl.when(jnp.logical_not(line_last))
+    def _():
+        pl.semaphore_signal(lower_ready, inc=1, device_id=device(row_at(line + 1), i), device_id_type=MESH)
+
+    def tell(place, carry):
+        pl.semaphore_signal(
+            upper_ready.at[line], inc=1, device_id=device(row_at(place), i), device_id_type=MESH
+        )
+        return carry
+
+    lax.fori_loop(0, line, tell, 0)
+
+    def give_row(row):
+        def give(k, carry):
+            place = lax.rem(i + k, cols)
+            send(
+                win.at[:, pl.ds(own, here), slice_of(place), head_columns(row)],
+                recv.at[:, mine],
+                row_send,
+                row_sem,
+                device(row, place),
+            ).start()
+            return carry
+
+        lax.fori_loop(0, cols, give, 0)
 
     def give_below(k, carry):
-        give_head(z - k)
-        return carry
-
-    half = rows // 2
-    near = jnp.minimum(z, half)
-    lax.fori_loop(1, near + 1, give_below, 0)
+        give_row(row_at(line - k))
+        return carry
+
+    near = jnp.minimum(line, rows // 2)
+
+    def give_near(k, carry):
+        give_row(row_at(line - near + k))
+        return carry
+
+    lax.fori_loop(0, near, give_near, 0)
 
     def relay(place):
         first, length = spans[place]
@@ -330,43 +371,18 @@
             pltpu.make_async_copy(span, span, cross_sem.at[place - (cols - 3)]).wait()
             relay(place).start()
 
-    lax.fori_loop(near + 1, z + 1, give_below, 0)
-
-    def give_above(row, carry):
-        pl.semaphore_wait(upper_ready.at[row], 1)
-        give_head(row)
-        return carry
-
-    lax.fori_loop(z + 1, rows, give_above, 0)
-
-    block_tables(counts_ref, tails_ref, order_ref, slots_ref, small_rows, table_vmem)
-
-    def arrived(step):
-        k = step // 2 + 1
-        row = lax.rem(z + jnp.where(lax.rem(step, 2) == 0, k, rows - k), rows)
-        pltpu.make_async_copy(stage.at[row], stage.at[row], z_sem.at[row]).wait()
-
-        def give(n, carry):
-            place = lax.rem(i + n, cols)
-            send(
-                stage.at[row, :, :, slice_of(place), :],
-                recv.at[:, blocks_of(row)],
-                row_send,
-                row_sem,
-                device(z, place),
-            ).start()
-            return carry
-
-        lax.fori_loop(1, cols, give, 0)
-        recv[:, blocks_of(row)] = stage[row, :, :, slice_of(i), :]
-
-    early = (rows - 1) // 2
-
-    def early_step(step, carry):
-        arrived(step)
-        return carry
-
-    lax.fori_loop(0, early, early_step, 0)
+    lax.fori_loop(near + 1, line + 1, give_below, 0)
+
+    def give_above(place, carry):
+        pl.semaphore_wait(upper_ready.at[place], 1)
+        give_row(row_at(place))
+        return carry
+
+    lax.fori_loop(line + 1, rows, give_above, 0)
+
+    for load in later:
+        load.wait()
+    block_tables(counts, tails, order, slots, small_rows, table_vmem)
 
     table_copy = pltpu.make_async_copy(table_vmem, table, table_sem)
     table_copy.start()
@@ -424,26 +440,13 @@
         mixed = jnp.dot(weights.astype(BF16), values, preferred_element_type=F32)
         att_ref[:, at] = jnp.where(query_ok, mixed / totals, 0.0).astype(BF16)
 
-    per_step = HEADS // (rows - 1 - early)
-
-    def late_step(step, carry):
-        def one(n, c):
-            attend((step - early) * per_step + n)
-            return c
-
-        lax.fori_loop(0, per_step, one, 0)
-        arrived(step)
-        return carry
-
-    lax.fori_loop(early, rows - 1, late_step, 0)
-
-    def rest(head, carry):
+    def attend_head(head, carry):
         attend(head)
         return carry
 
-    lax.fori_loop(per_step * (rows - 1 - early), HEADS, rest, 0)
-
-    landed = recv.at[:, pl.ds(0, rows * (cols - 1) * here)]
+    lax.fori_loop(0, HEADS, attend_head, 0)
+
+    landed = recv.at[:, pl.ds(0, (rows * cols - 1) * here)]
     pltpu.make_async_copy(landed, landed, row_sem).wait()
 
     def place_block(c, carry):
@@ -455,8 +458,6 @@
     lax.fori_loop(0, out_k.shape[0], place_block, 0, unroll=8)
 
     pltpu.make_async_copy(landed, landed, row_send).wait()
-    heads_sent = stage.at[pl.ds(0, rows - 1)]
-    pltpu.make_async_copy(heads_sent, heads_sent, z_send).wait()
     for place in spans:
 
         @pl.when(has_next & (i == place))
@@ -501,27 +502,28 @@
     attended, cache_keys, cache_values = pl.pallas_call(
         functools.partial(exchange_kernel, rows, cols),
         out_shape=[pltpu.VMEM(shape, BF16) for shape in shapes],
-        in_specs=[hbm] * 3 + [vmem] * 4,
+        in_specs=[hbm] * 7,
         out_specs=[vmem] * 3,
         scratch_shapes=[
             pltpu.VMEM((2, window, BLOCK, features), BF16),
             pltpu.VMEM((tokens, features), BF16),
-            pltpu.VMEM((rows, 2, here, BLOCK, HEAD_DIM), BF16),
             pltpu.VMEM((2, PRIOR, BLOCK, features // (cols // 2)), BF16),
             pltpu.VMEM((2, blocks, part, HEAD_DIM), BF16),
             pltpu.VMEM((tokens, window * BLOCK), F32),
+            pltpu.VMEM((1, prompts // 2), jnp.int32),
+            pltpu.VMEM((1, prompts), jnp.int32),
+            pltpu.VMEM((1, prompts), jnp.int32),
+            pltpu.VMEM((1, prompts // 2), jnp.int32),
             pltpu.VMEM((8, prompts), jnp.int32),
             pltpu.VMEM((8, blocks), jnp.int32),
             pltpu.SMEM((8, blocks), jnp.int32),
-            dma((3,)),
+            dma((7,)),
             dma,
             dma((2,)),
             dma((5,)),
             dma((3,)),
             dma((3, cols // 2)),
             dma((3,)),
-            dma,
-            dma((rows,)),
             dma,
             dma,
             regular,

time: 161 us -> 142 us (0.88)
  Pallas kernels: 156 us -> 136 us
    pallas_call x1, Pallas kernels: 156 us -> 136 us  [local(): pl.pallas_call(functools.partial(exchange_kernel, rows, cols), out_shape=...]
where the time goes in v2:
time: 142 us; the launch traced here: 140 us
  Pallas kernels  136 us (96%)
  local copies, waits for them, and re-layouts  2.91 us (2%)
    pallas_call x1, Pallas kernels, local(): pl.pallas_call(functools.partial(exchange_kernel, rows, cols), out_shape=...  136 us
    unnamed x3, local copies, waits for them, and re-layouts  2.91 us

profile of v2, /device:TPU:33, one launch (start us, length us, event | category | flops | bytes accessed | tf_op | source)
XLA Modules:
  0.0 140.1 jit_solution(523657833876875544)
XLA Ops:
  0.6 136.5 %shard_map.94 = (bf16[256,2048]{1,0:T(8,128)(2,1)S(1)}, bf16[256,16,128]{2,1,0:T(8,128)(2,1)S(1)}, bf16[256,16,128]{2,1,0:T(8,128)(2,1)S(1)}) custom-call(bf16[256,2048]{1,0:T(8,128)(2,1)} %q_ref.1, bf16[2,128,2048]{2,1,0:T(8,128)(2,1)} %bitcast.10, bf16[2,128,2048]{2,1,0:T(8,128)(2,1)} %bitcast.11, s32[1,64]{1,0:T(1,128)} %bitcast.12, s32[1,128]{1,0:T(1,128)} %bitcast.13, ...), custom_call_target="tpu_custom_call" | custom-call | tf_op jit(solution)/shard_map/pallas_call | solution.py:502
  137.1 1.0 copy.13
  138.1 1.0 copy.14
  139.1 1.0 copy.15

commit v3 on v2

--- a/solution.py
+++ b/solution.py
@@ -352,6 +352,15 @@
 
     lax.fori_loop(0, near, give_near, 0)
 
+    def give_above(place, carry):
+        pl.semaphore_wait(upper_ready.at[place], 1)
+        give_row(row_at(place))
+        return carry
+
+
+    first = jnp.minimum(line + 1 + 4, rows)
+    lax.fori_loop(line + 1, first, give_above, 0)
+
     def relay(place):
         first, length = spans[place]
         return send(
@@ -373,12 +382,7 @@
 
     lax.fori_loop(near + 1, line + 1, give_below, 0)
 
-    def give_above(place, carry):
-        pl.semaphore_wait(upper_ready.at[place], 1)
-        give_row(row_at(place))
-        return carry
-
-    lax.fori_loop(line + 1, rows, give_above, 0)
+    lax.fori_loop(first, rows, give_above, 0)
 
     for load in later:
         load.wait()

time: 142 us -> 144 us (1.014)
  the two profiles are of different devices: /device:TPU:33 before, /device:TPU:43 now
where the time goes in v3:
time: 144 us
  Pallas kernels  140 us (97%)
  local copies, waits for them, and re-layouts  2.91 us (2%)
    pallas_call x1, Pallas kernels, local(): pl.pallas_call(functools.partial(exchange_kernel, rows, cols), out_shape=...  140 us
    unnamed x3, local copies, waits for them, and re-layouts  2.91 us

profile of v3, /device:TPU:43, one launch (start us, length us, event | category | flops | bytes accessed | tf_op | source)
XLA Modules:
  0.0 143.6 jit_solution(15746297632132756495)
XLA Ops:
  0.6 140.0 %shard_map.94 = (bf16[256,2048]{1,0:T(8,128)(2,1)S(1)}, bf16[256,16,128]{2,1,0:T(8,128)(2,1)S(1)}, bf16[256,16,128]{2,1,0:T(8,128)(2,1)S(1)}) custom-call(bf16[256,2048]{1,0:T(8,128)(2,1)} %q_ref.1, bf16[2,128,2048]{2,1,0:T(8,128)(2,1)} %bitcast.10, bf16[2,128,2048]{2,1,0:T(8,128)(2,1)} %bitcast.11, s32[1,64]{1,0:T(1,128)} %bitcast.12, s32[1,128]{1,0:T(1,128)} %bitcast.13, ...), custom_call_target="tpu_custom_call" | custom-call | tf_op jit(solution)/shard_map/pallas_call | solution.py:506
  140.7 1.0 copy.13
  141.7 1.0 copy.14
  142.6 1.0 copy.15

commit v4 on v2

--- a/solution.py
+++ b/solution.py
@@ -444,7 +444,7 @@
         attend(head)
         return carry
 
-    lax.fori_loop(0, HEADS, attend_head, 0)
+    lax.fori_loop(0, HEADS, attend_head, 0, unroll=4)
 
     landed = recv.at[:, pl.ds(0, (rows * cols - 1) * here)]
     pltpu.make_async_copy(landed, landed, row_sem).wait()

time: 142 us -> 142 us (level)
  no operation moved by 1% of the time
where the time goes in v4:
time: 142 us; the launch traced here: 140 us
  Pallas kernels  136 us (96%)
  local copies, waits for them, and re-layouts  2.91 us (2%)
    pallas_call x1, Pallas kernels, local(): pl.pallas_call(functools.partial(exchange_kernel, rows, cols), out_shape=...  136 us
    unnamed x3, local copies, waits for them, and re-layouts  2.91 us

profile of v4, /device:TPU:33, one launch (start us, length us, event | category | flops | bytes accessed | tf_op | source)
XLA Modules:
  0.0 140.1 jit_solution(7197200256307233643)
XLA Ops:
  0.6 136.5 %shard_map.94 = (bf16[256,2048]{1,0:T(8,128)(2,1)S(1)}, bf16[256,16,128]{2,1,0:T(8,128)(2,1)S(1)}, bf16[256,16,128]{2,1,0:T(8,128)(2,1)S(1)}) custom-call(bf16[256,2048]{1,0:T(8,128)(2,1)} %q_ref.1, bf16[2,128,2048]{2,1,0:T(8,128)(2,1)} %bitcast.10, bf16[2,128,2048]{2,1,0:T(8,128)(2,1)} %bitcast.11, s32[1,64]{1,0:T(1,128)} %bitcast.12, s32[1,128]{1,0:T(1,128)} %bitcast.13, ...), custom_call_target="tpu_custom_call" | custom-call | tf_op jit(solution)/shard_map/pallas_call | solution.py:502
  137.1 1.0 copy.13
  138.1 1.0 copy.14
  139.1 1.0 copy.15
